TPU v7x, 32 devices: a whole 2x2x4 slice. The times are simulated.
32 devices in a mesh: dp: 8 (over y, x, core), seq: 4 (over z).
Axes of the slice: x: 2, y: 2, z: 4, core: 2. Of those that a mesh axis runs over, the one named last changes fastest.
Arguments:
- tokens: bfloat16 [16384, 1024], P(('dp', 'seq')), may hold values from -6 to 6
- cotangent: bfloat16 [16384, 1024], P(('dp', 'seq')), may hold values from -6 to 6
- qkv_weight: bfloat16 [1024, 3072], replicated, may hold values from -0.1875 to 0.1875
- proj_weight: bfloat16 [1024, 1024], replicated, may hold values from -0.75 to 0.75
- up_weight: bfloat16 [1024, 4096], replicated, may hold values from -0.1875 to 0.1875
- down_weight: bfloat16 [4096, 1024], replicated, may hold values from -0.09375 to 0.09375
- norm_gains: float32 [2, 1024], replicated, may hold values from 0.5 to 1.5
- biases: float32 [6, 1024], replicated, may hold values from -1.5 to 1.5
- up_bias: float32 [4096], replicated, may hold values from -1.5 to 1.5
- head_slopes: float32 [16], replicated, may hold values from 0.00012207031 to 0.5, as said below
- qkv_moment: float32 [1024, 3072], P(None, 'dp'), may hold values from -1536 to 1536
- proj_moment: float32 [1024, 1024], P(None, 'dp'), may hold values from -1536 to 1536
- up_moment: float32 [1024, 4096], P(None, 'dp'), may hold values from -1536 to 1536
- down_moment: float32 [4096, 1024], P('dp'), may hold values from -1536 to 1536
- gains_moment: float32 [2, 1024], P(None, 'dp'), may hold values from -768 to 768
- biases_moment: float32 [6, 1024], P(None, 'dp'), may hold values from -768 to 768
- upbias_moment: float32 [4096], P('dp'), may hold values from -768 to 768
Outputs:
- block_out: bfloat16 [16384, 1024], P(('dp', 'seq'))
- tokens_grad: float32 [16384, 1024], P(('dp', 'seq'))
- qkv_grad: float32 [1024, 3072], P(None, 'dp')
- proj_grad: float32 [1024, 1024], P(None, 'dp')
- up_grad: float32 [1024, 4096], P(None, 'dp')
- down_grad: float32 [4096, 1024], P('dp')
- gains_grad: float32 [2, 1024], P(None, 'dp')
- biases_grad: float32 [6, 1024], P(None, 'dp')
- upbias_grad: float32 [4096], P('dp')
- qkv_state: float32 [1024, 3072], P(None, 'dp')
- proj_state: float32 [1024, 1024], P(None, 'dp')
- up_state: float32 [1024, 4096], P(None, 'dp')
- down_state: float32 [4096, 1024], P('dp')
- gains_state: float32 [2, 1024], P(None, 'dp')
- biases_state: float32 [6, 1024], P(None, 'dp')
- upbias_state: float32 [4096], P('dp')
- qkv_new: float32 [1024, 3072], P(None, 'dp')
- proj_new: float32 [1024, 1024], P(None, 'dp')
- up_new: float32 [1024, 4096], P(None, 'dp')
- down_new: float32 [4096, 1024], P('dp')
- gains_new: float32 [2, 1024], P(None, 'dp')
- biases_new: float32 [6, 1024], P(None, 'dp')
- upbias_new: float32 [4096], P('dp')
Inputs may be any that keep to these rules, and one draw needn't show every extreme that they name: `head_slopes`: one positive slope a head.
All inputs are finite; a program needn't handle non-finite values.
Results may differ from a plain program's by a relative error of at most 0.025.
Values may be sent and summed in bfloat16 or wider, within the bound.
A program may use at most 256 MiB of HBM per device.

v0:
```python
import math
import jax
import jax.numpy as jnp
from jax import lax
from jax.sharding import PartitionSpec as P

NS_ITERS = 5
MOMENTUM = 0.9
RATE_MATRIX = 0.2
RATE_VECTOR = 0.0015
NORM_EPS = 1e-05
ORTHO_EPS = 1e-07
COEF_A = 2.0
COEF_B = -1.0
GELU_C = 0.7978845608028654
MASKED = -1e30


def norm_forward(values, gain_row, offset):
    center = values - jnp.mean(values, axis=-1, keepdims=True)
    inv_scale = lax.rsqrt(jnp.mean(center * center, axis=-1, keepdims=True) + NORM_EPS)
    unit_values = center * inv_scale
    return (unit_values * gain_row + offset, unit_values, inv_scale)


def norm_backward(upstream, unit_values, inv_scale, gain_row):
    scaled = upstream * gain_row
    inner_sum = jnp.mean(scaled * unit_values, axis=-1, keepdims=True)
    input_grad = inv_scale * (
        scaled - jnp.mean(scaled, axis=-1, keepdims=True) - unit_values * inner_sum
    )
    return (input_grad, jnp.sum(upstream * unit_values, axis=0), jnp.sum(upstream, axis=0))


def gelu_tanh(values):
    return 0.5 * values * (1.0 + jnp.tanh(GELU_C * (values + 0.044715 * values * values * values)))


def gelu_slope(values):
    tangent = jnp.tanh(GELU_C * (values + 0.044715 * values * values * values))
    return 0.5 * (1.0 + tangent) + 0.5 * values * (1.0 - tangent * tangent) * GELU_C * (
        1.0 + 3.0 * 0.044715 * values * values
    )


def contract_rows(left, right):
    return lax.dot_general(
        left, right, (((0,), (0,)), ((), ())), preferred_element_type=jnp.float32
    )


def contract_cols(left, right):
    return lax.dot_general(
        left, right, (((1,), (1,)), ((), ())), preferred_element_type=jnp.float32
    )


def split_heads(matrix, groups):
    row_count = matrix.shape[0]
    return jnp.moveaxis(matrix.reshape(row_count, groups, 2, -1), 1, 0)


def join_heads(stacked):
    row_count = stacked.shape[1]
    return jnp.moveaxis(stacked, 0, 1).reshape(row_count, -1)


def score_block(query_g, key_g, slope_g, distance, allowed):
    scale = 1.0 / math.sqrt(query_g.shape[-1])
    scores = jnp.einsum("qhd,khd->hqk", query_g, key_g, preferred_element_type=jnp.float32) * scale
    scores = scores - slope_g[:, None, None] * distance[None]
    return jnp.where(allowed[None], scores, MASKED)


def group_forward(items, distance, allowed):
    query_g, key_g, value_g, slope_g = items
    scores = score_block(query_g, key_g, slope_g, distance, allowed)
    peak_score = jnp.max(scores, axis=-1, keepdims=True)
    log_total = peak_score + jnp.log(jnp.sum(jnp.exp(scores - peak_score), axis=-1, keepdims=True))
    soft_weights = jnp.exp(scores - log_total).astype(jnp.bfloat16)
    attended = jnp.einsum("hqk,khd->qhd", soft_weights, value_g, preferred_element_type=jnp.float32)
    return (attended, log_total[..., 0])


def group_backward(items, distance, allowed):
    query_g, key_g, value_g, slope_g, log_total, upstream_g = items
    scale = 1.0 / math.sqrt(query_g.shape[-1])
    scores = score_block(query_g, key_g, slope_g, distance, allowed)
    chances = jnp.exp(scores - log_total[..., None])
    soft_weights = chances.astype(jnp.bfloat16)
    soft_grad = jnp.einsum("qhd,khd->hqk", upstream_g, value_g, preferred_element_type=jnp.float32)
    inner_sum = jnp.sum(soft_grad * chances, axis=-1, keepdims=True)
    score_grad = (chances * (soft_grad - inner_sum)).astype(jnp.bfloat16)
    query_grad = (
        jnp.einsum("hqk,khd->qhd", score_grad, key_g, preferred_element_type=jnp.float32) * scale
    ).astype(jnp.bfloat16)
    key_grad = (
        jnp.einsum("hqk,qhd->khd", score_grad, query_g, preferred_element_type=jnp.float32) * scale
    )
    value_grad = jnp.einsum(
        "hqk,qhd->khd", soft_weights, upstream_g, preferred_element_type=jnp.float32
    )
    return (query_grad, key_grad, value_grad)


def on_device(
    tokens,
    cotangent,
    qkv_weight,
    proj_weight,
    up_weight,
    down_weight,
    norm_gains,
    biases,
    up_bias,
    head_slopes,
    qkv_moment,
    proj_moment,
    up_moment,
    down_moment,
    gains_moment,
    biases_moment,
    upbias_moment,
):
    row_count, model_width = tokens.shape
    groups = head_slopes.shape[0] // 2
    seq_length = row_count * lax.axis_size("seq")
    positions = lax.axis_index("seq") * row_count + jnp.arange(row_count, dtype=jnp.int32)
    key_index = jnp.arange(seq_length, dtype=jnp.int32)
    distance = (positions[:, None] - key_index[None, :]).astype(jnp.float32)
    allowed = key_index[None, :] <= positions[:, None]
    slopes = head_slopes.reshape(groups, 2)
    inputs = tokens.astype(jnp.float32)
    normed_one, unit_one, scale_one = norm_forward(inputs, norm_gains[0], biases[0])
    normed_one = normed_one.astype(jnp.bfloat16)
    mixed = jnp.dot(normed_one, qkv_weight, preferred_element_type=jnp.float32)
    queries = (mixed[:, :model_width] + biases[1]).astype(jnp.bfloat16)
    key_part = mixed[:, model_width : 2 * model_width].astype(jnp.bfloat16)
    value_part = (mixed[:, 2 * model_width :] + biases[2]).astype(jnp.bfloat16)
    key_rows, value_rows = (
        lax.all_gather(key_part, "seq", axis=0, tiled=True),
        lax.all_gather(value_part, "seq", axis=0, tiled=True),
    )
    query_groups = split_heads(queries, groups)
    key_groups = split_heads(key_rows, groups)
    value_groups = split_heads(value_rows, groups)

    def forward_group(items):
        return group_forward(items, distance, allowed)

    attended, log_totals = lax.map(forward_group, (query_groups, key_groups, value_groups, slopes))
    mixed_heads = join_heads(attended).astype(jnp.bfloat16)
    middle = (
        inputs + jnp.dot(mixed_heads, proj_weight, preferred_element_type=jnp.float32) + biases[3]
    )
    normed_two, unit_two, scale_two = norm_forward(middle, norm_gains[1], biases[4])
    normed_two = normed_two.astype(jnp.bfloat16)
    before = jnp.dot(normed_two, up_weight, preferred_element_type=jnp.float32) + up_bias
    hidden = gelu_tanh(before).astype(jnp.bfloat16)
    block_out = (
        middle + jnp.dot(hidden, down_weight, preferred_element_type=jnp.float32) + biases[5]
    ).astype(jnp.bfloat16)
    upstream = cotangent.astype(jnp.float32)
    down_grad = contract_rows(cotangent, hidden)
    hidden_grad = contract_cols(cotangent, down_weight)
    before_grad = (hidden_grad * gelu_slope(before)).astype(jnp.bfloat16)
    up_grad = contract_rows(normed_two, before_grad)
    normed_two_grad = contract_cols(before_grad, up_weight)
    middle_back, gain_two_grad, offset_two_grad = norm_backward(
        normed_two_grad, unit_two, scale_two, norm_gains[1]
    )
    middle_grad = upstream + middle_back
    branch_grad = middle_grad.astype(jnp.bfloat16)
    proj_grad = contract_rows(mixed_heads, branch_grad)
    heads_grad = contract_cols(branch_grad, proj_weight).astype(jnp.bfloat16)

    def backward_group(items):
        return group_backward(items, distance, allowed)

    query_grad, key_grad, value_grad = lax.map(
        backward_group,
        (
            query_groups,
            key_groups,
            value_groups,
            slopes,
            log_totals,
            split_heads(heads_grad, groups),
        ),
    )
    query_grad = join_heads(query_grad)
    key_sum, value_sum = (
        lax.psum_scatter(
            join_heads(key_grad).astype(jnp.bfloat16), "seq", scatter_dimension=0, tiled=True
        ).astype(jnp.float32),
        lax.psum_scatter(
            join_heads(value_grad).astype(jnp.bfloat16), "seq", scatter_dimension=0, tiled=True
        ).astype(jnp.float32),
    )
    key_low = key_sum.astype(jnp.bfloat16)
    value_low = value_sum.astype(jnp.bfloat16)
    mixed_grad = jnp.concatenate([query_grad, key_low, value_low], axis=1)
    qkv_grad = contract_rows(normed_one, mixed_grad)
    normed_one_grad = contract_cols(mixed_grad, qkv_weight)
    input_back, gain_one_grad, offset_one_grad = norm_backward(
        normed_one_grad, unit_one, scale_one, norm_gains[0]
    )
    tokens_grad = middle_grad + input_back
    gains_grad = jnp.stack([gain_one_grad, gain_two_grad])
    biases_grad = jnp.stack(
        [
            offset_one_grad,
            jnp.sum(query_grad.astype(jnp.float32), axis=0),
            jnp.sum(value_low.astype(jnp.float32), axis=0),
            jnp.sum(branch_grad.astype(jnp.float32), axis=0),
            offset_two_grad,
            jnp.sum(upstream, axis=0),
        ]
    )
    upbias_grad = jnp.sum(before_grad.astype(jnp.float32), axis=0)[None]
    qkv_part, proj_part, up_part, down_part, gains_part, biases_part, upbias_part = (
        lax.psum_scatter(
            qkv_grad.astype(jnp.bfloat16), "dp", scatter_dimension=1, tiled=True
        ).astype(jnp.float32),
        lax.psum_scatter(
            proj_grad.astype(jnp.bfloat16), "dp", scatter_dimension=1, tiled=True
        ).astype(jnp.float32),
        lax.psum_scatter(
            up_grad.astype(jnp.bfloat16), "dp", scatter_dimension=1, tiled=True
        ).astype(jnp.float32),
        lax.psum_scatter(
            down_grad.astype(jnp.bfloat16), "dp", scatter_dimension=1, tiled=True
        ).astype(jnp.float32),
        lax.psum_scatter(
            gains_grad.astype(jnp.bfloat16), "dp", scatter_dimension=1, tiled=True
        ).astype(jnp.float32),
        lax.psum_scatter(
            biases_grad.astype(jnp.bfloat16), "dp", scatter_dimension=1, tiled=True
        ).astype(jnp.float32),
        lax.psum_scatter(
            upbias_grad.astype(jnp.bfloat16), "dp", scatter_dimension=1, tiled=True
        ).astype(jnp.float32),
    )
    qkv_sum, proj_sum, up_sum, down_sum, gains_sum, biases_sum, upbias_sum = (
        lax.psum(qkv_part.astype(jnp.bfloat16), "seq").astype(jnp.float32),
        lax.psum(proj_part.astype(jnp.bfloat16), "seq").astype(jnp.float32),
        lax.psum(up_part.astype(jnp.bfloat16), "seq").astype(jnp.float32),
        lax.psum(down_part.astype(jnp.bfloat16), "seq").astype(jnp.float32),
        lax.psum(gains_part.astype(jnp.bfloat16), "seq").astype(jnp.float32),
        lax.psum(biases_part.astype(jnp.bfloat16), "seq").astype(jnp.float32),
        lax.psum(upbias_part.astype(jnp.bfloat16), "seq").astype(jnp.float32),
    )
    qkv_state = MOMENTUM * qkv_moment + qkv_sum
    proj_state = MOMENTUM * proj_moment + proj_sum
    up_state = MOMENTUM * up_moment + up_sum
    down_oriented = MOMENTUM * down_moment.T + down_sum
    gains_state = MOMENTUM * gains_moment + gains_sum
    biases_state = MOMENTUM * biases_moment + biases_sum
    upbias_state = MOMENTUM * upbias_moment + upbias_sum[0]
    oriented = (qkv_state, proj_state, up_state, down_oriented)
    pad_width = max((member.shape[1] for member in oriented))
    stacked = jnp.stack(
        [
            jnp.pad(member.astype(jnp.bfloat16), ((0, 0), (0, pad_width - member.shape[1])))
            for member in oriented
        ]
    )
    owned_block = lax.dynamic_index_in_dim(stacked, lax.axis_index("seq"), 0, keepdims=False)
    iterate = owned_block
    for iteration in range(NS_ITERS):
        gram = lax.psum(contract_cols(iterate, iterate).astype(jnp.bfloat16), "dp").astype(
            jnp.float32
        )
        if iteration == 0:
            factor = 1.0 / (jnp.sqrt(jnp.trace(gram)) + ORTHO_EPS)
            square = gram * factor * factor
            iterate = (owned_block.astype(jnp.float32) * factor).astype(jnp.bfloat16)
        else:
            square = gram
        square_low = square.astype(jnp.bfloat16)
        iterate = (
            COEF_A * iterate.astype(jnp.float32)
            + COEF_B * jnp.dot(square_low, iterate, preferred_element_type=jnp.float32)
        ).astype(jnp.bfloat16)
    shared = lax.all_gather(iterate[None], "seq", axis=0, tiled=True)

    def step_of(slot_number, column_count, whole_shape):
        return (
            -RATE_MATRIX
            * math.sqrt(max(whole_shape[0], whole_shape[1]))
            * shared[slot_number][:, :column_count].astype(jnp.float32)
        )

    dp_index = lax.axis_index("dp")

    def own_cols(matrix, count):
        return lax.dynamic_slice_in_dim(matrix, dp_index * count, count, 1).astype(jnp.float32)

    qkv_new = own_cols(qkv_weight, qkv_state.shape[1]) + step_of(
        0, qkv_state.shape[1], qkv_weight.shape
    )
    proj_new = own_cols(proj_weight, proj_state.shape[1]) + step_of(
        1, proj_state.shape[1], proj_weight.shape
    )
    up_new = own_cols(up_weight, up_state.shape[1]) + step_of(2, up_state.shape[1], up_weight.shape)
    down_count = down_oriented.shape[1]
    down_rows = lax.dynamic_slice_in_dim(down_weight, dp_index * down_count, down_count, 0).astype(
        jnp.float32
    )
    down_new = down_rows + step_of(3, down_count, down_weight.shape).T
    gains_new = own_cols(norm_gains, gains_state.shape[1]) - RATE_VECTOR * gains_state
    biases_new = own_cols(biases, biases_state.shape[1]) - RATE_VECTOR * biases_state
    upbias_count = upbias_state.shape[0]
    upbias_new = (
        lax.dynamic_slice_in_dim(up_bias, dp_index * upbias_count, upbias_count, 0)
        - RATE_VECTOR * upbias_state
    )
    return (
        block_out,
        tokens_grad,
        qkv_sum,
        proj_sum,
        up_sum,
        down_sum.T,
        gains_sum,
        biases_sum,
        upbias_sum[0],
        qkv_state,
        proj_state,
        up_state,
        down_oriented.T,
        gains_state,
        biases_state,
        upbias_state,
        qkv_new,
        proj_new,
        up_new,
        down_new,
        gains_new,
        biases_new,
        upbias_new,
    )


def solution(mesh):
    placed = (
        P(("dp", "seq"), None),
        P(("dp", "seq"), None),
        P(),
        P(),
        P(),
        P(),
        P(),
        P(),
        P(),
        P(),
        P(None, "dp"),
        P(None, "dp"),
        P(None, "dp"),
        P("dp", None),
        P(None, "dp"),
        P(None, "dp"),
        P("dp"),
    )
    return jax.shard_map(
        on_device,
        mesh=mesh,
        in_specs=placed,
        out_specs=(
            P(("dp", "seq"), None),
            P(("dp", "seq"), None),
            P(None, "dp"),
            P(None, "dp"),
            P(None, "dp"),
            P("dp", None),
            P(None, "dp"),
            P(None, "dp"),
            P("dp"),
            P(None, "dp"),
            P(None, "dp"),
            P(None, "dp"),
            P("dp", None),
            P(None, "dp"),
            P(None, "dp"),
            P("dp"),
            P(None, "dp"),
            P(None, "dp"),
            P(None, "dp"),
            P("dp", None),
            P(None, "dp"),
            P(None, "dp"),
            P("dp"),
        ),
        check_vma=False,
    )
```

profile of v0, /device:TPU:0, one launch (start us, length us, event | category | flops | bytes accessed | tf_op | source)
XLA Modules:
  0.0 1661.3 jit_solution(17056713743389701598)
XLA Ops:
  12.8 6.1 fusion.105
  26.7 78.8 %all-gather.5.cloned.1.call-done = bf16[2048,1024]{1,0:T(8,128)(2,1)} async-done(((bf16[512,1024]{1,0:T(8,128)(2,1)}), bf16[2048,1024]{1,0:T(8,128)(2,1)}) %all-gather.5.cloned.1.call-update) | async-done | bytes 4194320 | tf_op jit(solution)/shard_map/all_gather | solution.py:142
  105.5 6.5 copy.60
  112.0 74.9 %all-gather.7.cloned.1.call-done = bf16[2048,1024]{1,0:T(8,128)(2,1)} async-done(((bf16[512,1024]{1,0:T(8,128)(2,1)}), bf16[2048,1024]{1,0:T(8,128)(2,1)}) %all-gather.7.cloned.1.call-update) | async-done | bytes 4194320 | tf_op jit(solution)/shard_map/all_gather | solution.py:141
  186.9 6.5 copy.62
  193.4 102.7 %while.30 = (s32[]{:T(128)}, bf16[8,512,2,64]{1,3,2,0:T(8,128)(2,1)}, f32[8,2,512]{2,1,0:T(2,128)S(1)}, bf16[8,2048,2,64]{1,3,2,0:T(8,128)(2,1)}, bf16[8,512,2,6...) while((s32[]{:T(128)}, ...), condition=%wide.region_5.6_spmd.clone.clone, body=%wide.region_2.5_spmd.clone.clone.sunk | while | flops 575667200 | bytes 47618196 | solution.py:151
  201.7 4.5 fusion.167
  214.5 4.5 fusion.167
  220.1 4.0 fusion.166
  227.4 4.5 fusion.167
  240.2 4.5 fusion.167
  253.0 4.5 fusion.167
  265.9 4.5 fusion.167
  278.7 4.5 fusion.167
  291.5 4.5 fusion.167
  299.1 10.7 fusion.107
  309.8 13.6 fusion.113
  323.4 5.7 multiply_reduce_fusion.1
  334.6 222.8 %while.31 = (s32[]{:T(128)}, bf16[8,512,2,64]{1,3,2,0:T(8,128)(2,1)}, bf16[8,2048,2,64]{1,3,2,0:T(8,128)(2,1)}, bf16[8,2048,2,64]{1,3,2,0:T(8,128)(2,1)}, bf16[8...) while((s32[]{:T(128)}, ...), condition=%wide.region_12.13_spmd.clone.clone, body=%wide.region_10.12_spmd.clone.clone.sunk | while | flops 1368783872 | bytes 144864496 | solution.py:180
  343.3 5.7 multiply_reduce_fusion.7
  349.0 6.6 multiply_convert_fusion.7
  371.1 5.7 multiply_reduce_fusion.7
  376.8 6.6 multiply_convert_fusion.7
  391.5 4.0 subtract_exponential_fusion.2
  398.9 5.7 multiply_reduce_fusion.7
  404.6 6.6 multiply_convert_fusion.7
  419.3 4.0 subtract_exponential_fusion.2
  426.7 5.7 multiply_reduce_fusion.7
  432.4 6.6 multiply_convert_fusion.7
  454.5 5.7 multiply_reduce_fusion.7
  460.3 6.6 multiply_convert_fusion.7
  482.4 5.7 multiply_reduce_fusion.7
  488.1 6.6 multiply_convert_fusion.7
  510.2 5.7 multiply_reduce_fusion.7
  515.9 6.6 multiply_convert_fusion.7
  530.6 4.0 subtract_exponential_fusion.2
  538.0 5.7 multiply_reduce_fusion.7
  543.7 6.6 multiply_convert_fusion.7
  561.8 4.3 copy.73
  566.6 66.1 %reduce-scatter.20.cloned.1.call-done = bf16[512,1024]{0,1:T(8,128)(2,1)} async-done(((bf16[2048,1024]{0,1:T(8,128)(2,1)}), bf16[512,1024]{0,1:T(8,128)(2,1)}) %reduce-scatter.20.cloned.1.call-update) | async-done | bytes 1048592 | tf_op jit(solution)/shard_map/reduce_scatter | solution.py:193
  632.7 79.5 %reduce-scatter.22.cloned.1.call-done = bf16[512,1024]{0,1:T(8,128)(2,1)} async-done(((bf16[2048,1024]{0,1:T(8,128)(2,1)}), bf16[512,1024]{0,1:T(8,128)(2,1)}) %reduce-scatter.22.cloned.1.call-update) | async-done | bytes 1048592 | tf_op jit(solution)/shard_map/reduce_scatter | solution.py:196
  712.2 8.1 convolution_convert_fusion.1
  720.3 8.6 copy.71
  730.2 11.4 convert_bitcast_fusion
  743.2 9.2 convolution_convert_fusion
  752.7 4.9 reduce-scatter.30.cloned.1.call-done
  759.4 63.2 %reduce-scatter.28.cloned.1.call-done = bf16[384,1024]{1,0:T(8,128)(2,1)} async-done(((bf16[3072,1024]{1,0:T(8,128)(2,1)}), bf16[384,1024]{1,0:T(8,128)(2,1)}) %reduce-scatter.28.cloned.1.call-update) | async-done | bytes 786448
  824.9 72.5 %reduce-scatter.26.cloned.1.call-done = bf16[1024,512]{1,0:T(8,128)(2,1)} async-done(((bf16[1024,4096]{1,0:T(8,128)(2,1)}), bf16[1024,512]{1,0:T(8,128)(2,1)}) %reduce-scatter.26.cloned.1.call-update) | async-done | bytes 1048592 | tf_op jit(solution)/shard_map/reduce_scatter | solution.py:231
  897.4 74.8 %reduce-scatter.24.cloned.1.call-done = bf16[1024,512]{1,0:T(8,128)(2,1)} async-done(((bf16[1024,4096]{1,0:T(8,128)(2,1)}), bf16[1024,512]{1,0:T(8,128)(2,1)}) %reduce-scatter.24.cloned.1.call-update) | async-done | bytes 1048592 | tf_op jit(solution)/shard_map/reduce_scatter | solution.py:228
  975.1 121.9 %all-reduce.21.cloned.1.call-done = (bf16[1024,384]{1,0:T(8,128)(2,1)}, bf16[1024,128]{1,0:T(8,128)(2,1)}, bf16[1024,512]{1,0:T(8,128)(2,1)}, bf16[1024,512]{1,0:T(8,128)(2,1)}) async-done(((bf16[1024,384]{1,0:T(8,128)(2,1)}, bf16[1024,128]{1,0:T(8,128)(2,1)}, bf16[1024,512]{1,0:T(8,128)(2,1)}, bf16[1024,512]{1,0:T(8,128)(2,1)}), (bf16[1024,384]{1,0:T(8,128)(2,1)}, bf16[1024,128]{1,0:T(8,128)(2,1)}, ...) | async-done | bytes 3145744 | tf_op jit(solution)/shard_map/psum | solution.py:245
  1112.3 60.9 %all-reduce.11.cloned.1.call-done = bf16[1024,1024]{1,0:T(8,128)(2,1)} async-done(((bf16[1024,1024]{1,0:T(8,128)(2,1)}), bf16[1024,1024]{1,0:T(8,128)(2,1)}) %all-reduce.11.cloned.1.call-update) | async-done | bytes 2097168 | tf_op jit(solution)/shard_map/psum | solution.py:271
  1183.4 60.9 %all-reduce.13.cloned.1.call-done = bf16[1024,1024]{1,0:T(8,128)(2,1)} async-done(((bf16[1024,1024]{1,0:T(8,128)(2,1)}), bf16[1024,1024]{1,0:T(8,128)(2,1)}) %all-reduce.13.cloned.1.call-update) | async-done | bytes 2097168 | tf_op jit(solution)/shard_map/psum | solution.py:271
  1251.4 60.9 %all-reduce.15.cloned.1.call-done = bf16[1024,1024]{1,0:T(8,128)(2,1)} async-done(((bf16[1024,1024]{1,0:T(8,128)(2,1)}), bf16[1024,1024]{1,0:T(8,128)(2,1)}) %all-reduce.15.cloned.1.call-update) | async-done | bytes 2097168 | tf_op jit(solution)/shard_map/psum | solution.py:271
  1319.5 60.9 %all-reduce.17.cloned.1.call-done = bf16[1024,1024]{1,0:T(8,128)(2,1)} async-done(((bf16[1024,1024]{1,0:T(8,128)(2,1)}), bf16[1024,1024]{1,0:T(8,128)(2,1)}) %all-reduce.17.cloned.1.call-update) | async-done | bytes 2097168 | tf_op jit(solution)/shard_map/psum | solution.py:271
  1389.4 9.4 fusion.80
  1404.0 44.5 %all-reduce.19.cloned.1.call-done = bf16[1024,1024]{1,0:T(8,128)(2,1)} async-done(((bf16[1024,1024]{1,0:T(8,128)(2,1)}), bf16[1024,1024]{1,0:T(8,128)(2,1)}) %all-reduce.19.cloned.1.call-update) | async-done | bytes 2097168 | tf_op jit(solution)/shard_map/psum | solution.py:271
  1448.5 4.4 add_convert_fusion
  1457.5 12.6 add_convert_fusion.5
  1470.1 17.1 %reduce-scatter.36.cloned.1.call-done = bf16[512,1]{1,0:T(8,128)(2,1)} async-done(((bf16[4096,1]{1,0:T(8,128)(2,1)}), bf16[512,1]{1,0:T(8,128)(2,1)}) %reduce-scatter.36.cloned.1.call-update) | async-done | bytes 1040
  1488.3 4.2 fusion.79
  1492.5 31.8 %reduce-scatter.32.cloned.1.call-done = bf16[128,2]{1,0:T(8,128)(2,1)} async-done(((bf16[1024,2]{1,0:T(8,128)(2,1)}), bf16[128,2]{1,0:T(8,128)(2,1)}) %reduce-scatter.32.cloned.1.call-update) | async-done | bytes 528
  1525.2 35.7 %reduce-scatter.34.cloned.1.call-done = bf16[128,6]{1,0:T(8,128)(2,1)} async-done(((bf16[1024,6]{1,0:T(8,128)(2,1)}), bf16[128,6]{1,0:T(8,128)(2,1)}) %reduce-scatter.34.cloned.1.call-update) | async-done | bytes 1552
  1561.7 11.8 all-reduce.2
  1584.4 58.7 %all-gather.9.cloned.1.call-done = bf16[4096,512]{1,0:T(8,128)(2,1)} async-done(((bf16[1024,512]{1,0:T(8,128)(2,1)}), bf16[4096,512]{1,0:T(8,128)(2,1)}) %all-gather.9.cloned.1.call-update) | async-done | bytes 4194320 | tf_op jit(solution)/shard_map/all_gather | solution.py:285
  (369 shorter events, 292.4 us)
Async XLA Ops:
  7.2 98.3 %all-gather.5.cloned.1.call-start = ((), (), s32[]{:S(2)}) async-start(), calls=%async_computation.9 | async-start | bytes 5242880 | tf_op jit(solution)/shard_map/all_gather | solution.py:142
  8.7 10.2 copy-start.24
  10.3 8.5 copy-start.31
  11.1 7.7 copy-start.26
  12.7 6.1 copy-start.36
  12.8 286.3 %copy-start.34 = (f32[1,1024]{1,0:T(1,128)}, f32[1,1024]{1,0:T(1,128)S(1)}, u32[]{:S(2)}) copy-start(f32[1,1024]{1,0:T(1,128)S(1)} %get-tuple-element.393) | copy-start | bytes 12292
  21.8 3.4 copy-start.43
  21.9 165.0 %all-gather.7.cloned.1.call-start = ((), (), s32[]{:S(2)}) async-start(), calls=%async_computation.10 | async-start | bytes 5242880 | tf_op jit(solution)/shard_map/all_gather | solution.py:141
  24.7 608.1 %reduce-scatter.20.cloned.1.call-start = ((), (), s32[]{:S(2)}) async-start(), calls=%async_computation.11 | async-start | bytes 5242880 | tf_op jit(solution)/shard_map/reduce_scatter | solution.py:193
  193.4 102.7 %copy-start.3 = (bf16[512,1024]{1,0:T(8,128)(2,1)S(1)}, bf16[512,1024]{1,0:T(8,128)(2,1)}, u32[]{:S(2)}) copy-start(bf16[512,1024]{1,0:T(8,128)(2,1)} %param.21) | copy-start | bytes 3145732
  193.4 102.7 %copy-start.14 = (bf16[1024,1024]{1,0:T(8,128)(2,1)S(1)}, bf16[1024,1024]{1,0:T(8,128)(2,1)}, u32[]{:S(2)}) copy-start(bf16[1024,1024]{1,0:T(8,128)(2,1)} %param.24) | copy-start | bytes 6291460
  298.6 30.4 %copy-start.1 = (f32[512,1024]{1,0:T(8,128)}, f32[512,1024]{1,0:T(8,128)S(1)}, u32[]{:S(2)}) copy-start(f32[512,1024]{1,0:T(8,128)S(1)} %get-tuple-element.402) | copy-start | bytes 6291460
  299.0 10.8 copy-start.17
  299.0 10.8 copy-start.44
  299.0 24.3 %slice-start = ((s8[8388608]{0:T(1024)(128)(4,1)}), s8[4194304]{0:T(1024)(128)(4,1)S(1)}, s32[]{:S(2)}) async-start(s8[8388608]{0:T(1024)(128)(4,1)} %bitcast.226), calls=%async_computation.27 | async-start | bytes 8388608
  309.8 13.6 slice-start.1
  323.4 5.7 copy-start.49
  339.9 3.4 copy-start
  355.6 3.3 copy-start.10
  367.7 3.4 copy-start
  383.4 3.3 copy-start.10
  395.5 3.4 copy-start
  411.2 3.3 copy-start.10
  423.3 3.4 copy-start
  439.0 3.3 copy-start.10
  451.1 3.4 copy-start
  466.8 3.3 copy-start.10
  478.9 3.4 copy-start
  494.7 3.3 copy-start.10
  506.8 3.4 copy-start
  522.5 3.3 copy-start.10
  534.6 3.4 copy-start
  550.3 3.3 copy-start.10
  557.4 154.8 %reduce-scatter.22.cloned.1.call-start = ((), (), s32[]{:S(2)}) async-start(), calls=%async_computation.12 | async-start | bytes 5242880 | tf_op jit(solution)/shard_map/reduce_scatter | solution.py:196
  558.0 199.6 %reduce-scatter.30.cloned.1.call-start = ((), (), s32[]{:S(2)}) async-start(), calls=%async_computation.22 | async-start | bytes 2359296
  561.8 150.4 %copy-start.4 = (bf16[512,1024]{1,0:T(8,128)(2,1)S(1)}, bf16[512,1024]{1,0:T(8,128)(2,1)}, u32[]{:S(2)}) copy-start(bf16[512,1024]{1,0:T(8,128)(2,1)} %param.21) | copy-start | bytes 3145732
  561.8 150.4 %copy-start.19 = (bf16[8,512,2,64]{1,3,2,0:T(8,128)(2,1)S(1)}, bf16[8,512,2,64]{1,3,2,0:T(8,128)(2,1)}, u32[]{:S(2)}) copy-start(bf16[8,512,2,64]{1,3,2,0:T(8,128)(2,1)} %get-tuple-element.137) | copy-start | bytes 3145732
  561.8 150.4 %copy-start.25 = (f32[512]{0:T(512)S(1)}, f32[512]{0:T(512)}, u32[]{:S(2)}) copy-start(f32[512]{0:T(512)} %copy-done.24) | copy-start | bytes 6148
  561.8 150.4 %copy-start.27 = (f32[1,1024]{1,0:T(1,128)S(1)}, f32[1,1024]{1,0:T(1,128)}, u32[]{:S(2)}) copy-start(f32[1,1024]{1,0:T(1,128)} %copy-done.26) | copy-start | bytes 12292
  561.8 150.4 %copy-start.32 = (f32[512]{0:T(512)S(1)}, f32[512]{0:T(512)}, u32[]{:S(2)}) copy-start(f32[512]{0:T(512)} %copy-done.31) | copy-start | bytes 6148
  561.8 150.4 %copy-start.37 = (f32[1,1024]{1,0:T(1,128)S(1)}, f32[1,1024]{1,0:T(1,128)}, u32[]{:S(2)}) copy-start(f32[1,1024]{1,0:T(1,128)} %copy-done.36) | copy-start | bytes 12292
  566.1 256.4 %reduce-scatter.28.cloned.1.call-start = ((), (), s32[]{:S(2)}) async-start(), calls=%async_computation.21 | async-start | bytes 7077888
  729.0 168.4 %reduce-scatter.26.cloned.1.call-start = ((), (), s32[]{:S(2)}) async-start(), calls=%async_computation.14 | async-start | bytes 9437184 | tf_op jit(solution)/shard_map/reduce_scatter | solution.py:231
  741.6 230.6 %reduce-scatter.24.cloned.1.call-start = ((), (), s32[]{:S(2)}) async-start(), calls=%async_computation.13 | async-start | bytes 9437184 | tf_op jit(solution)/shard_map/reduce_scatter | solution.py:228
  752.5 344.6 %all-reduce.21.cloned.1.call-start = ((), (), s32[]{:S(2)}) async-start(), calls=%async_computation.26 | async-start | bytes 6291456 | tf_op jit(solution)/shard_map/psum | solution.py:245
  972.2 200.9 %all-reduce.11.cloned.1.call-start = ((), (), s32[]{:S(2)}) async-start(), calls=%async_computation.15 | async-start | bytes 4194304 | tf_op jit(solution)/shard_map/psum | solution.py:271
  1099.5 3.0 copy-start.12
  1112.2 132.2 %all-reduce.13.cloned.1.call-start = ((), (), s32[]{:S(2)}) async-start(), calls=%async_computation.16 | async-start | bytes 4194304 | tf_op jit(solution)/shard_map/psum | solution.py:271
  1183.4 129.0 %all-reduce.15.cloned.1.call-start = ((), (), s32[]{:S(2)}) async-start(), calls=%async_computation.17 | async-start | bytes 4194304 | tf_op jit(solution)/shard_map/psum | solution.py:271
  1251.4 129.0 %all-reduce.17.cloned.1.call-start = ((), (), s32[]{:S(2)}) async-start(), calls=%async_computation.18 | async-start | bytes 4194304 | tf_op jit(solution)/shard_map/psum | solution.py:271
  1319.4 129.1 %all-reduce.19.cloned.1.call-start = ((), (), s32[]{:S(2)}) async-start(), calls=%async_computation.19 | async-start | bytes 4194304 | tf_op jit(solution)/shard_map/psum | solution.py:271
  1387.5 99.7 %reduce-scatter.36.cloned.1.call-start = ((), (), s32[]{:S(2)}) async-start(), calls=%async_computation.25 | async-start | bytes 1179648
  1389.1 12.2 copy-start.39
  1389.2 12.2 copy-start.30
  1389.2 12.2 copy-start.29
  1389.2 135.2 %reduce-scatter.32.cloned.1.call-start = ((), (), s32[]{:S(2)}) async-start(), calls=%async_computation.23 | async-start | bytes 294912
  1399.8 161.1 %reduce-scatter.34.cloned.1.call-start = ((), (), s32[]{:S(2)}) async-start(), calls=%async_computation.24 | async-start | bytes 294912
  1403.9 239.2 %all-gather.9.cloned.1.call-start = ((), (), s32[]{:S(2)}) async-start(), calls=%async_computation.20 | async-start | bytes 5242880 | tf_op jit(solution)/shard_map/all_gather | solution.py:285
  1452.9 4.6 copy-start.33
  1488.2 85.3 %copy-start.42 = (f32[2,128]{1,0:T(2,128)S(1)}, f32[2,128]{1,0:T(2,128)}, u32[]{:S(2)}) copy-start(f32[2,128]{1,0:T(2,128)} %param.35) | copy-start | bytes 3076
  1488.2 86.5 %copy-start.41 = (f32[512]{0:T(512)S(1)}, f32[512]{0:T(512)}, u32[]{:S(2)}) copy-start(f32[512]{0:T(512)} %param.37) | copy-start | bytes 6148
  1488.3 87.2 %copy-start.38 = (f32[6,128]{1,0:T(8,128)S(1)}, f32[6,128]{1,0:T(8,128)}, u32[]{:S(2)}) copy-start(f32[6,128]{1,0:T(8,128)} %param.36) | copy-start | bytes 9220
  1576.7 5.9 copy-start.5
  1582.6 60.5 %copy-start.13 = (bf16[512,1024]{0,1:T(8,128)(2,1)S(1)}, bf16[512,1024]{0,1:T(8,128)(2,1)}, u32[]{:S(2)}) copy-start(bf16[512,1024]{0,1:T(8,128)(2,1)} %copy.81) | copy-start | bytes 3145732
  (27 other events, 50.7 us)
Sparse Core Ops, SparseCore 0:
  22.0 83.4 all-gather.4
  107.6 79.2 all-gather.6
  557.5 75.1 reduce-scatter.19
  634.9 77.2 reduce-scatter.21
  715.9 41.6 reduce-scatter.29
  760.8 61.7 reduce-scatter.27
  826.0 71.3 reduce-scatter.25
  900.9 71.2 reduce-scatter.23
  976.0 121.0 all-reduce.20
  1112.3 60.7 all-reduce.10
  1183.5 60.8 all-reduce.12
  1251.5 60.8 all-reduce.14
  1319.6 60.8 all-reduce.16
  1387.6 60.8 all-reduce.18
  1452.1 35.0 reduce-scatter.35
  1490.6 33.6 reduce-scatter.31
  1527.2 33.6 reduce-scatter.33
  1562.3 80.7 all-gather.8
where the time goes:
time: 1670 us; the launch traced here: 1660 us
  waiting for transfers between devices  1070 us (64%)
  matrix products  337 us (20%)
  other arithmetic  136 us (8%)
  local copies, waits for them, and re-layouts  88.3 us (5%)
    psum x5, waiting for transfers between devices, on_device(): lax.psum(contract_cols(iterate, iterate).astype(jnp.bfloat16), 'dp')  288 us
    unnamed x23, waiting for transfers between devices  154 us
    psum x1, waiting for transfers between devices, on_device(): lax.psum(qkv_part.astype(jnp.bfloat16), 'seq').astype(jnp.float32)  122 us
    reduce_scatter x1, waiting for transfers between devices, on_device(): lax.psum_scatter(join_heads(value_grad).astype(jnp.bfloat16), 'seq', scat...  79.5 us
    all_gather x1, waiting for transfers between devices, on_device(): lax.all_gather(value_part, 'seq', axis=0, tiled=True)  78.8 us
    all_gather x1, waiting for transfers between devices, on_device(): lax.all_gather(key_part, 'seq', axis=0, tiled=True)  74.9 us
    reduce_scatter x1, waiting for transfers between devices, on_device(): lax.psum_scatter(up_grad.astype(jnp.bfloat16), 'dp', scatter_dimension=1,...  74.8 us
    reduce_scatter x1, waiting for transfers between devices, on_device(): lax.psum_scatter(down_grad.astype(jnp.bfloat16), 'dp', scatter_dimension=...  72.5 us
  transfers between devices with their start and end apart: 18, of which 18 were waited for; matrix products, arithmetic and copies ran while one was open for 7% of the time, Pallas kernels for 0%

commit v1 on v0

--- a/solution.py
+++ b/solution.py
@@ -14,6 +14,18 @@
 COEF_B = -1.0
 GELU_C = 0.7978845608028654
 MASKED = -1e30
+
+
+def collect(shard, axis, dim):
+    ways, here = (lax.axis_size(axis), lax.axis_index(axis))
+    grown, reach = (shard, 1)
+    while reach < ways:
+        theirs = lax.ppermute(grown, axis, [(d, d ^ reach) for d in range(ways)])
+        mine_first = jnp.concatenate([grown, theirs], axis=dim)
+        theirs_first = jnp.concatenate([theirs, grown], axis=dim)
+        grown = jnp.where(here & reach == 0, mine_first, theirs_first)
+        reach = 2 * reach
+    return grown
 
 
 def norm_forward(values, gain_row, offset):
@@ -139,7 +151,7 @@
     value_part = (mixed[:, 2 * model_width :] + biases[2]).astype(jnp.bfloat16)
     key_rows, value_rows = (
         lax.all_gather(key_part, "seq", axis=0, tiled=True),
-        lax.all_gather(value_part, "seq", axis=0, tiled=True),
+        collect(value_part, "seq", 0),
     )
     query_groups = split_heads(queries, groups)
     key_groups = split_heads(key_rows, groups)

time: 1670 us -> 1690 us (1.012)
    ppermute x0 -> x2, waiting for transfers between devices: none -> 159 us  [collect(): theirs = lax.ppermute(grown, axis, [(d, d ^ reach) for d in range(ways)])]
    all_gather x1 -> x0, waiting for transfers between devices: 78.8 us -> none  [on_device(): lax.all_gather(value_part, 'seq', axis=0, tiled=True)]
    all_gather x1, waiting for transfers between devices: 74.9 us -> 0.01 us  [on_device(): lax.all_gather(key_part, 'seq', axis=0, tiled=True)]
    unnamed x23 -> x22, waiting for transfers between devices: 154 us -> 154 us
  transfers between devices with their start and end apart: 18 -> 19, of which waited for: 18 -> 18; matrix products, arithmetic and copies ran while one was open for 7% -> 8% of each run, Pallas kernels for 0% -> 0%
where the time goes in v1:
time: 1690 us
  waiting for transfers between devices  1070 us (63%)
  matrix products  337 us (20%)
  other arithmetic  147 us (9%)
  local copies, waits for them, and re-layouts  88.8 us (5%)
    psum x5, waiting for transfers between devices, on_device(): lax.psum(contract_cols(iterate, iterate).astype(jnp.bfloat16), 'dp')  288 us
    ppermute x2, waiting for transfers between devices, collect(): theirs = lax.ppermute(grown, axis, [(d, d ^ reach) for d in range(ways)])  159 us
    unnamed x22, waiting for transfers between devices  154 us
    psum x1, waiting for transfers between devices, on_device(): lax.psum(qkv_part.astype(jnp.bfloat16), 'seq').astype(jnp.float32)  122 us
    reduce_scatter x1, waiting for transfers between devices, on_device(): lax.psum_scatter(join_heads(value_grad).astype(jnp.bfloat16), 'seq', scat...  79.6 us
    reduce_scatter x1, waiting for transfers between devices, on_device(): lax.psum_scatter(up_grad.astype(jnp.bfloat16), 'dp', scatter_dimension=1,...  74.8 us
    reduce_scatter x1, waiting for transfers between devices, on_device(): lax.psum_scatter(down_grad.astype(jnp.bfloat16), 'dp', scatter_dimension=...  72.4 us
    reduce_scatter x1, waiting for transfers between devices, on_device(): lax.psum_scatter(join_heads(key_grad).astype(jnp.bfloat16), 'seq', scatte...  66.7 us
  transfers between devices with their start and end apart: 19, of which 18 were waited for; matrix products, arithmetic and copies ran while one was open for 8% of the time, Pallas kernels for 0%

profile of v1, /device:TPU:0, one launch (start us, length us, event | category | flops | bytes accessed | tf_op | source)
XLA Modules:
  0.0 1687.5 jit_solution(9207747525896104789)
XLA Ops:
  12.8 6.1 fusion.106
  29.6 71.1 %collective-permute-done = bf16[512,1024]{1,0:T(8,128)(2,1)S(1)} collective-permute-done((bf16[512,1024]{1,0:T(8,128)(2,1)S(1)}, bf16[512,1024]{1,0:T(8,128)(2,1)S(1)}, u32[]{:S(2)}, u32[]{:S(2)}) %collective-permute-start) | collective-permute-done | bytes 1048608 | tf_op jit(solution)/shard_map/ppermute | solution.py:23
  103.0 6.3 collective-permute-start.1
  116.3 87.8 %collective-permute-done.1 = bf16[1024,1024]{1,0:T(8,128)(2,1)} collective-permute-done((bf16[1024,1024]{1,0:T(8,128)(2,1)}, bf16[1024,1024]{1,0:T(8,128)(2,1)}, u32[]{:S(2)}, u32[]{:S(2)}) %collective-permute-start.1) | collective-permute-done | bytes 2097184 | tf_op jit(solution)/shard_map/ppermute | solution.py:23
  208.1 5.1 fusion.68
  213.2 6.4 copy.71
  219.7 102.7 %while.30 = (s32[]{:T(128)}, bf16[8,512,2,64]{1,3,2,0:T(8,128)(2,1)}, f32[8,2,512]{2,1,0:T(2,128)S(1)}, bf16[8,2048,2,64]{1,3,2,0:T(8,128)(2,1)}, bf16[8,512,2,6...) while((s32[]{:T(128)}, ...), condition=%wide.region_5.6_spmd.clone.clone, body=%wide.region_2.5_spmd.clone.clone.sunk | while | flops 575667200 | bytes 47618196 | solution.py:163
  228.0 4.5 fusion.168
  240.8 4.5 fusion.168
  246.4 4.0 fusion.167
  253.7 4.5 fusion.168
  266.5 4.5 fusion.168
  272.0 4.0 fusion.167
  279.3 4.5 fusion.168
  284.9 4.0 fusion.167
  292.2 4.5 fusion.168
  305.0 4.5 fusion.168
  317.8 4.5 fusion.168
  325.4 10.7 fusion.108
  336.1 13.5 fusion.114
  349.7 5.7 multiply_reduce_fusion.1
  360.9 222.5 %while.31 = (s32[]{:T(128)}, bf16[8,512,2,64]{1,3,2,0:T(8,128)(2,1)}, bf16[8,2048,2,64]{1,3,2,0:T(8,128)(2,1)}, bf16[8,2048,2,64]{1,3,2,0:T(8,128)(2,1)}, bf16[8...) while((s32[]{:T(128)}, ...), condition=%wide.region_12.13_spmd.clone.clone, body=%wide.region_10.12_spmd.clone.clone.sunk | while | flops 1368783872 | bytes 144864496 | solution.py:192
  369.6 5.7 multiply_reduce_fusion.7
  375.3 6.6 multiply_convert_fusion.7
  397.3 5.7 multiply_reduce_fusion.7
  403.1 6.6 multiply_convert_fusion.7
  425.1 5.7 multiply_reduce_fusion.7
  430.9 6.6 multiply_convert_fusion.7
  452.9 5.7 multiply_reduce_fusion.7
  458.6 6.6 multiply_convert_fusion.7
  480.7 5.7 multiply_reduce_fusion.7
  486.4 6.6 multiply_convert_fusion.7
  508.5 5.7 multiply_reduce_fusion.7
  514.2 6.6 multiply_convert_fusion.7
  536.3 5.7 multiply_reduce_fusion.7
  542.0 6.6 multiply_convert_fusion.7
  564.1 5.7 multiply_reduce_fusion.7
  569.8 6.6 multiply_convert_fusion.7
  587.9 4.3 copy.82
  592.6 66.7 %reduce-scatter.20.cloned.1.call-done = bf16[512,1024]{0,1:T(8,128)(2,1)} async-done(((bf16[2048,1024]{0,1:T(8,128)(2,1)}), bf16[512,1024]{0,1:T(8,128)(2,1)}) %reduce-scatter.20.cloned.1.call-update) | async-done | bytes 1048592 | tf_op jit(solution)/shard_map/reduce_scatter | solution.py:205
  659.3 79.6 %reduce-scatter.22.cloned.1.call-done = bf16[512,1024]{0,1:T(8,128)(2,1)} async-done(((bf16[2048,1024]{0,1:T(8,128)(2,1)}), bf16[512,1024]{0,1:T(8,128)(2,1)}) %reduce-scatter.22.cloned.1.call-update) | async-done | bytes 1048592 | tf_op jit(solution)/shard_map/reduce_scatter | solution.py:208
  739.0 8.1 convolution_convert_fusion.1
  747.0 8.7 copy.80
  756.9 11.4 convert_bitcast_fusion
  770.0 9.2 convolution_convert_fusion
  779.5 4.9 reduce-scatter.30.cloned.1.call-done
  786.1 63.2 %reduce-scatter.28.cloned.1.call-done = bf16[384,1024]{1,0:T(8,128)(2,1)} async-done(((bf16[3072,1024]{1,0:T(8,128)(2,1)}), bf16[384,1024]{1,0:T(8,128)(2,1)}) %reduce-scatter.28.cloned.1.call-update) | async-done | bytes 786448
  851.6 72.4 %reduce-scatter.26.cloned.1.call-done = bf16[1024,512]{1,0:T(8,128)(2,1)} async-done(((bf16[1024,4096]{1,0:T(8,128)(2,1)}), bf16[1024,512]{1,0:T(8,128)(2,1)}) %reduce-scatter.26.cloned.1.call-update) | async-done | bytes 1048592 | tf_op jit(solution)/shard_map/reduce_scatter | solution.py:243
  924.0 74.8 %reduce-scatter.24.cloned.1.call-done = bf16[1024,512]{1,0:T(8,128)(2,1)} async-done(((bf16[1024,4096]{1,0:T(8,128)(2,1)}), bf16[1024,512]{1,0:T(8,128)(2,1)}) %reduce-scatter.24.cloned.1.call-update) | async-done | bytes 1048592 | tf_op jit(solution)/shard_map/reduce_scatter | solution.py:240
  1001.7 121.9 %all-reduce.21.cloned.1.call-done = (bf16[1024,384]{1,0:T(8,128)(2,1)}, bf16[1024,128]{1,0:T(8,128)(2,1)}, bf16[1024,512]{1,0:T(8,128)(2,1)}, bf16[1024,512]{1,0:T(8,128)(2,1)}) async-done(((bf16[1024,384]{1,0:T(8,128)(2,1)}, bf16[1024,128]{1,0:T(8,128)(2,1)}, bf16[1024,512]{1,0:T(8,128)(2,1)}, bf16[1024,512]{1,0:T(8,128)(2,1)}), (bf16[1024,384]{1,0:T(8,128)(2,1)}, bf16[1024,128]{1,0:T(8,128)(2,1)}, ...) | async-done | bytes 3145744 | tf_op jit(solution)/shard_map/psum | solution.py:257
  1138.8 60.9 %all-reduce.11.cloned.1.call-done = bf16[1024,1024]{1,0:T(8,128)(2,1)} async-done(((bf16[1024,1024]{1,0:T(8,128)(2,1)}), bf16[1024,1024]{1,0:T(8,128)(2,1)}) %all-reduce.11.cloned.1.call-update) | async-done | bytes 2097168 | tf_op jit(solution)/shard_map/psum | solution.py:283
  1210.0 60.9 %all-reduce.13.cloned.1.call-done = bf16[1024,1024]{1,0:T(8,128)(2,1)} async-done(((bf16[1024,1024]{1,0:T(8,128)(2,1)}), bf16[1024,1024]{1,0:T(8,128)(2,1)}) %all-reduce.13.cloned.1.call-update) | async-done | bytes 2097168 | tf_op jit(solution)/shard_map/psum | solution.py:283
  1278.0 60.9 %all-reduce.15.cloned.1.call-done = bf16[1024,1024]{1,0:T(8,128)(2,1)} async-done(((bf16[1024,1024]{1,0:T(8,128)(2,1)}), bf16[1024,1024]{1,0:T(8,128)(2,1)}) %all-reduce.15.cloned.1.call-update) | async-done | bytes 2097168 | tf_op jit(solution)/shard_map/psum | solution.py:283
  1346.1 60.9 %all-reduce.17.cloned.1.call-done = bf16[1024,1024]{1,0:T(8,128)(2,1)} async-done(((bf16[1024,1024]{1,0:T(8,128)(2,1)}), bf16[1024,1024]{1,0:T(8,128)(2,1)}) %all-reduce.17.cloned.1.call-update) | async-done | bytes 2097168 | tf_op jit(solution)/shard_map/psum | solution.py:283
  1416.0 9.4 fusion.81
  1430.6 44.5 %all-reduce.19.cloned.1.call-done = bf16[1024,1024]{1,0:T(8,128)(2,1)} async-done(((bf16[1024,1024]{1,0:T(8,128)(2,1)}), bf16[1024,1024]{1,0:T(8,128)(2,1)}) %all-reduce.19.cloned.1.call-update) | async-done | bytes 2097168 | tf_op jit(solution)/shard_map/psum | solution.py:283
  1475.0 4.4 add_convert_fusion
  1484.0 12.6 add_convert_fusion.5
  1496.6 17.1 %reduce-scatter.36.cloned.1.call-done = bf16[512,1]{1,0:T(8,128)(2,1)} async-done(((bf16[4096,1]{1,0:T(8,128)(2,1)}), bf16[512,1]{1,0:T(8,128)(2,1)}) %reduce-scatter.36.cloned.1.call-update) | async-done | bytes 1040
  1514.8 4.2 fusion.80
  1519.0 31.8 %reduce-scatter.32.cloned.1.call-done = bf16[128,2]{1,0:T(8,128)(2,1)} async-done(((bf16[1024,2]{1,0:T(8,128)(2,1)}), bf16[128,2]{1,0:T(8,128)(2,1)}) %reduce-scatter.32.cloned.1.call-update) | async-done | bytes 528
  1551.7 35.8 %reduce-scatter.34.cloned.1.call-done = bf16[128,6]{1,0:T(8,128)(2,1)} async-done(((bf16[1024,6]{1,0:T(8,128)(2,1)}), bf16[128,6]{1,0:T(8,128)(2,1)}) %reduce-scatter.34.cloned.1.call-update) | async-done | bytes 1552
  1588.3 11.8 all-reduce.2
  1610.9 58.7 %all-gather.6.cloned.1.call-done = bf16[4096,512]{1,0:T(8,128)(2,1)} async-done(((bf16[1024,512]{1,0:T(8,128)(2,1)}), bf16[4096,512]{1,0:T(8,128)(2,1)}) %all-gather.6.cloned.1.call-update) | async-done | bytes 4194320 | tf_op jit(solution)/shard_map/all_gather | solution.py:297
  (375 shorter events, 312.6 us)
Async XLA Ops:
  7.2 206.1 %all-gather.4.cloned.1.call-start = ((), (), s32[]{:S(2)}) async-start(), calls=%async_computation.9 | async-start | bytes 5242880 | tf_op jit(solution)/shard_map/all_gather | solution.py:153
  8.7 10.2 copy-start.24
  10.3 8.5 copy-start.31
  11.1 7.7 copy-start.26
  12.7 6.1 copy-start.36
  12.8 312.6 %copy-start.34 = (f32[1,1024]{1,0:T(1,128)}, f32[1,1024]{1,0:T(1,128)S(1)}, u32[]{:S(2)}) copy-start(f32[1,1024]{1,0:T(1,128)S(1)} %get-tuple-element.393) | copy-start | bytes 12292
  22.7 636.6 %reduce-scatter.20.cloned.1.call-start = ((), (), s32[]{:S(2)}) async-start(), calls=%async_computation.10 | async-start | bytes 5242880 | tf_op jit(solution)/shard_map/reduce_scatter | solution.py:205
  26.5 74.1 %collective-permute-start = (bf16[512,1024]{1,0:T(8,128)(2,1)S(1)}, bf16[512,1024]{1,0:T(8,128)(2,1)S(1)}, u32[]{:S(2)}, u32[]{:S(2)}) collective-permute-start(bf16[512,1024]{1,0:T(8,128)(2,1)S(1)} %get-tuple-element.389), channel_id=1, source_target_pairs={{0,1},{1,0},{2,3},{3,2},{4,5},{5,4},{6,7},{7,6},{8,9},{9,8},{10,11... | collective-permute-start | bytes 3145736 | tf_op jit(solution)/shard_map/ppermute | solution.py:23
  29.6 80.7 %copy-start.43 = (f32[16]{0:T(128)S(1)}, f32[16]{0:T(128)}, u32[]{:S(2)}) copy-start(f32[16]{0:T(128)} %param.30) | copy-start | bytes 196
  103.0 101.2 %collective-permute-start.1 = (bf16[1024,1024]{1,0:T(8,128)(2,1)}, bf16[1024,1024]{1,0:T(8,128)(2,1)}, u32[]{:S(2)}, u32[]{:S(2)}) collective-permute-start(bf16[1024,1024]{1,0:T(8,128)(2,1)} %maximum_select_fusion.2), channel_id=1, source_target_pairs={{0,2},{1,3},{2,0},{3,1},{4,6},{5,7},{6,4},{7,5},{8,10},{9,11},{10,... | collective-permute-start | bytes 6291464 | tf_op jit(solution)/shard_map/ppermute | solution.py:23
  219.7 102.7 %copy-start.3 = (bf16[512,1024]{1,0:T(8,128)(2,1)S(1)}, bf16[512,1024]{1,0:T(8,128)(2,1)}, u32[]{:S(2)}) copy-start(bf16[512,1024]{1,0:T(8,128)(2,1)} %param.21) | copy-start | bytes 3145732
  219.7 102.7 %copy-start.14 = (bf16[1024,1024]{1,0:T(8,128)(2,1)S(1)}, bf16[1024,1024]{1,0:T(8,128)(2,1)}, u32[]{:S(2)}) copy-start(bf16[1024,1024]{1,0:T(8,128)(2,1)} %param.24) | copy-start | bytes 6291460
  325.0 30.4 %copy-start.1 = (f32[512,1024]{1,0:T(8,128)}, f32[512,1024]{1,0:T(8,128)S(1)}, u32[]{:S(2)}) copy-start(f32[512,1024]{1,0:T(8,128)S(1)} %get-tuple-element.402) | copy-start | bytes 6291460
  325.3 10.8 copy-start.17
  325.4 10.8 copy-start.44
  325.4 24.3 %slice-start = ((s8[8388608]{0:T(1024)(128)(4,1)}), s8[4194304]{0:T(1024)(128)(4,1)S(1)}, s32[]{:S(2)}) async-start(s8[8388608]{0:T(1024)(128)(4,1)} %bitcast.230), calls=%async_computation.26 | async-start | bytes 8388608
  336.1 13.6 slice-start.1
  349.7 5.7 copy-start.49
  366.1 3.4 copy-start
  381.9 3.3 copy-start.10
  394.0 3.4 copy-start
  409.6 3.3 copy-start.10
  421.7 3.4 copy-start
  437.4 3.3 copy-start.10
  449.5 3.4 copy-start
  465.2 3.3 copy-start.10
  477.3 3.4 copy-start
  493.0 3.3 copy-start.10
  505.1 3.4 copy-start
  520.8 3.3 copy-start.10
  532.9 3.4 copy-start
  548.6 3.3 copy-start.10
  560.7 3.4 copy-start
  576.3 3.3 copy-start.10
  583.4 155.5 %reduce-scatter.22.cloned.1.call-start = ((), (), s32[]{:S(2)}) async-start(), calls=%async_computation.11 | async-start | bytes 5242880 | tf_op jit(solution)/shard_map/reduce_scatter | solution.py:208
  584.2 200.1 %reduce-scatter.30.cloned.1.call-start = ((), (), s32[]{:S(2)}) async-start(), calls=%async_computation.21 | async-start | bytes 2359296
  587.9 151.1 %copy-start.4 = (bf16[512,1024]{1,0:T(8,128)(2,1)S(1)}, bf16[512,1024]{1,0:T(8,128)(2,1)}, u32[]{:S(2)}) copy-start(bf16[512,1024]{1,0:T(8,128)(2,1)} %param.21) | copy-start | bytes 3145732
  587.9 151.1 %copy-start.19 = (bf16[8,512,2,64]{1,3,2,0:T(8,128)(2,1)S(1)}, bf16[8,512,2,64]{1,3,2,0:T(8,128)(2,1)}, u32[]{:S(2)}) copy-start(bf16[8,512,2,64]{1,3,2,0:T(8,128)(2,1)} %get-tuple-element.137) | copy-start | bytes 3145732
  587.9 151.1 %copy-start.25 = (f32[512]{0:T(512)S(1)}, f32[512]{0:T(512)}, u32[]{:S(2)}) copy-start(f32[512]{0:T(512)} %copy-done.24) | copy-start | bytes 6148
  587.9 151.1 %copy-start.27 = (f32[1,1024]{1,0:T(1,128)S(1)}, f32[1,1024]{1,0:T(1,128)}, u32[]{:S(2)}) copy-start(f32[1,1024]{1,0:T(1,128)} %copy-done.26) | copy-start | bytes 12292
  587.9 151.1 %copy-start.32 = (f32[512]{0:T(512)S(1)}, f32[512]{0:T(512)}, u32[]{:S(2)}) copy-start(f32[512]{0:T(512)} %copy-done.31) | copy-start | bytes 6148
  587.9 151.1 %copy-start.37 = (f32[1,1024]{1,0:T(1,128)S(1)}, f32[1,1024]{1,0:T(1,128)}, u32[]{:S(2)}) copy-start(f32[1,1024]{1,0:T(1,128)} %copy-done.36) | copy-start | bytes 12292
  592.2 257.2 %reduce-scatter.28.cloned.1.call-start = ((), (), s32[]{:S(2)}) async-start(), calls=%async_computation.20 | async-start | bytes 7077888
  755.7 168.3 %reduce-scatter.26.cloned.1.call-start = ((), (), s32[]{:S(2)}) async-start(), calls=%async_computation.13 | async-start | bytes 9437184 | tf_op jit(solution)/shard_map/reduce_scatter | solution.py:243
  768.4 230.4 %reduce-scatter.24.cloned.1.call-start = ((), (), s32[]{:S(2)}) async-start(), calls=%async_computation.12 | async-start | bytes 9437184 | tf_op jit(solution)/shard_map/reduce_scatter | solution.py:240
  779.2 344.4 %all-reduce.21.cloned.1.call-start = ((), (), s32[]{:S(2)}) async-start(), calls=%async_computation.25 | async-start | bytes 6291456 | tf_op jit(solution)/shard_map/psum | solution.py:257
  998.8 200.9 %all-reduce.11.cloned.1.call-start = ((), (), s32[]{:S(2)}) async-start(), calls=%async_computation.14 | async-start | bytes 4194304 | tf_op jit(solution)/shard_map/psum | solution.py:283
  1138.8 132.2 %all-reduce.13.cloned.1.call-start = ((), (), s32[]{:S(2)}) async-start(), calls=%async_computation.15 | async-start | bytes 4194304 | tf_op jit(solution)/shard_map/psum | solution.py:283
  1210.0 129.0 %all-reduce.15.cloned.1.call-start = ((), (), s32[]{:S(2)}) async-start(), calls=%async_computation.16 | async-start | bytes 4194304 | tf_op jit(solution)/shard_map/psum | solution.py:283
  1278.0 129.0 %all-reduce.17.cloned.1.call-start = ((), (), s32[]{:S(2)}) async-start(), calls=%async_computation.17 | async-start | bytes 4194304 | tf_op jit(solution)/shard_map/psum | solution.py:283
  1346.0 129.0 %all-reduce.19.cloned.1.call-start = ((), (), s32[]{:S(2)}) async-start(), calls=%async_computation.18 | async-start | bytes 4194304 | tf_op jit(solution)/shard_map/psum | solution.py:283
  1414.1 99.7 %reduce-scatter.36.cloned.1.call-start = ((), (), s32[]{:S(2)}) async-start(), calls=%async_computation.24 | async-start | bytes 1179648
  1415.7 12.2 copy-start.39
  1415.8 12.2 copy-start.30
  1415.8 12.2 copy-start.29
  1415.8 135.1 %reduce-scatter.32.cloned.1.call-start = ((), (), s32[]{:S(2)}) async-start(), calls=%async_computation.22 | async-start | bytes 294912
  1426.4 161.0 %reduce-scatter.34.cloned.1.call-start = ((), (), s32[]{:S(2)}) async-start(), calls=%async_computation.23 | async-start | bytes 294912
  1430.5 239.1 %all-gather.6.cloned.1.call-start = ((), (), s32[]{:S(2)}) async-start(), calls=%async_computation.19 | async-start | bytes 5242880 | tf_op jit(solution)/shard_map/all_gather | solution.py:297
  1479.4 4.6 copy-start.33
  1514.8 85.3 %copy-start.42 = (f32[2,128]{1,0:T(2,128)S(1)}, f32[2,128]{1,0:T(2,128)}, u32[]{:S(2)}) copy-start(f32[2,128]{1,0:T(2,128)} %param.35) | copy-start | bytes 3076
  1514.8 86.5 %copy-start.41 = (f32[512]{0:T(512)S(1)}, f32[512]{0:T(512)}, u32[]{:S(2)}) copy-start(f32[512]{0:T(512)} %param.37) | copy-start | bytes 6148
  1514.8 87.2 %copy-start.38 = (f32[6,128]{1,0:T(8,128)S(1)}, f32[6,128]{1,0:T(8,128)}, u32[]{:S(2)}) copy-start(f32[6,128]{1,0:T(8,128)} %param.36) | copy-start | bytes 9220
  1603.2 5.9 copy-start.5
  1609.1 60.5 %copy-start.13 = (bf16[512,1024]{0,1:T(8,128)(2,1)S(1)}, bf16[512,1024]{0,1:T(8,128)(2,1)}, u32[]{:S(2)}) copy-start(bf16[512,1024]{0,1:T(8,128)(2,1)} %copy.90) | copy-start | bytes 3145732
  (28 other events, 53.3 us)
Sparse Core Ops, SparseCore 0:
  22.8 110.4 all-gather.3
  583.5 75.7 reduce-scatter.19
  661.6 77.2 reduce-scatter.21
  742.7 41.6 reduce-scatter.29
  787.5 61.7 reduce-scatter.27
  852.7 71.2 reduce-scatter.25
  927.4 71.2 reduce-scatter.23
  1002.5 121.0 all-reduce.20
  1138.9 60.7 all-reduce.10
  1210.1 60.8 all-reduce.12
  1278.1 60.8 all-reduce.14
  1346.1 60.8 all-reduce.16
  1414.2 60.8 all-reduce.18
  1478.6 35.0 reduce-scatter.35
  1517.2 33.6 reduce-scatter.31
  1553.7 33.6 reduce-scatter.33
  1588.8 80.7 all-gather.5
